TPU v7x, 32 devices: a whole 2x2x4 slice. The times are simulated.
32 devices in a mesh: row: 8 (over y, x, core), col: 4 (over z).
Axes of the slice: x: 2, y: 2, z: 4, core: 2. Of those that a mesh axis runs over, the one named last changes fastest.
Arguments:
- band_tiles: bfloat16 [8, 64, 256, 256], P('row', 'col'), may hold values from 0.0009994507 to 1
- band_cell: int32 [8, 64], P('row', 'col'), may hold values from 0 to 63, as said below
- band_count: int32 [8, 4], P('row', 'col'), may hold values from 1 to 16, as said below
- matrix_tiles: bfloat16 [8, 64, 256, 256], P('row', 'col'), may hold values from 7.390976e-05 to 0.07421875
- matrix_col: int32 [8, 64], P('row', 'col'), may hold values from 0 to 31
- matrix_live: int32 [8, 64], P('row', 'col'), may hold values 0 or 1
Outputs:
- reached: bfloat16 [4096, 32768], P('row', 'col')
- gained: float32 [], replicated
Inputs may be any that keep to these rules, and one draw needn't show every extreme that they name: The band_cell values of one device's 16 slots are distinct. `band_count`: among the 4 devices of one index of row, the live slots with slot number 16 // 2 or more number at most 8 in all.
All inputs are finite; a program needn't handle non-finite values. No bound on the sum of `matrix_live` on one device may be relied on, other than what follows from the above.
Results may differ from a plain program's by a relative error of at most 0.001.
Values may be sent and summed in bfloat16 or wider, within the bound.
No kernel may reach another device: no remote copies, remote signals or barrier semaphores. Data moves between devices by JAX's collectives and lax.ppermute only.
A program may use at most 128 MiB of HBM per device.

v0:
```python
import jax
import jax.numpy as jnp
from jax import lax
from jax.sharding import PartitionSpec as P

TILES = 128
BR = 2


def on_device(band_tiles, band_cell, band_count, matrix_tiles, matrix_col, matrix_live):
    slots_own = band_tiles.shape[1]
    tile = band_tiles.shape[-1]
    n_col = lax.axis_size("col")
    tcols = TILES // n_col
    places = BR * tcols
    spots = jnp.arange(places, dtype=jnp.int32)
    b_tiles, b_index, b_live = (
        lax.all_gather(matrix_tiles, "row", axis=0, tiled=True),
        lax.all_gather(matrix_col, "row", axis=0, tiled=True),
        lax.all_gather(matrix_live, "row", axis=0, tiled=True),
    )
    flat_tiles = b_tiles.reshape(-1, tile, tile)
    half = slots_own // 2
    front_tiles, a_cell, a_count = (
        lax.all_gather(band_tiles[:, :half], "col", axis=1, tiled=True),
        lax.all_gather(band_cell, "col", axis=1, tiled=True),
        lax.all_gather(band_count, "col", axis=1, tiled=True),
    )
    counts = a_count[0]
    spill = jnp.maximum(counts - half, 0)
    before = jnp.cumsum(spill) - spill
    ending = before + spill
    mine = lax.axis_index("col")
    own_before = jnp.take(before, mine)
    own_spill = jnp.maximum(band_count[0, 0] - half, 0)
    pack_spot = jnp.arange(half, dtype=jnp.int32)
    upper = jnp.arange(half, dtype=jnp.int32)
    place_w = (
        (pack_spot[:, None] == own_before + upper[None, :]) & (upper[None, :] < own_spill)
    ).astype(jnp.bfloat16)
    packed = jnp.einsum(
        "qs,sxy->qxy", place_w, band_tiles[0, half:], preferred_element_type=jnp.float32
    )
    spilled = lax.psum(packed.astype(jnp.bfloat16), "col")
    holder = jnp.sum((ending[None, :] <= pack_spot[:, None]).astype(jnp.int32), axis=1)
    holder = jnp.clip(holder, 0, n_col - 1)
    spill_slot = jnp.clip(half + pack_spot - jnp.take(before, holder), 0, slots_own - 1)
    spill_cell = jnp.take(a_cell[0], holder * slots_own + spill_slot)
    spill_valid = pack_spot < jnp.sum(spill)
    front = jnp.arange(n_col * half, dtype=jnp.int32)
    front_source = front // half
    front_slot = front % half
    front_cell = jnp.take(a_cell[0], front_source * slots_own + front_slot)
    front_valid = front_slot < jnp.take(counts, front_source)
    sources = jnp.concatenate([front_source, holder])
    cells = jnp.concatenate([front_cell, spill_cell])
    valid = jnp.concatenate([front_valid, spill_valid])
    tiles = jnp.concatenate([front_tiles[0], spilled], axis=0)
    k_glob = sources * tcols + cells % tcols
    i_loc = cells // tcols
    picked = jnp.take(flat_tiles, k_glob, axis=0)
    picked_index = jnp.take(b_index.reshape(-1), k_glob)
    picked_live = jnp.take(b_live.reshape(-1), k_glob)
    live = (picked_live > 0) & valid
    position = i_loc * tcols + picked_index
    product = jnp.einsum("axy,ayz->axz", tiles, picked, preferred_element_type=jnp.float32)
    weights = ((position[:, None] == spots[None, :]) & live[:, None]).astype(jnp.float32)
    summed = jnp.einsum("ap,axz->pxz", weights, product, precision=lax.Precision.HIGHEST)
    own_live = jnp.arange(slots_own, dtype=jnp.int32) < band_count[0, 0]
    own_w = ((band_cell[0][:, None] == spots[None, :]) & own_live[:, None]).astype(jnp.bfloat16)
    base = jnp.einsum("sp,sxz->pxz", own_w, band_tiles[0], preferred_element_type=jnp.float32)
    expanded = jnp.minimum(1.0, base + summed)
    block = (
        expanded.reshape(BR, tcols, tile, tile)
        .transpose(0, 2, 1, 3)
        .reshape(BR * tile, tcols * tile)
    )
    total = lax.psum(jnp.sum(expanded - base), ("row", "col"))
    devices = lax.axis_size("row") * n_col
    gained = total / (tile * tile * devices * places)
    return (block.astype(jnp.bfloat16), gained)


def solution(mesh):
    in_specs = (
        P("row", "col", None, None),
        P("row", "col"),
        P("row", "col"),
        P("row", "col", None, None),
        P("row", "col"),
        P("row", "col"),
    )
    out_specs = (P("row", "col"), P())
    return jax.shard_map(
        on_device, mesh=mesh, in_specs=in_specs, out_specs=out_specs, check_vma=False
    )
```

profile of v0, /device:TPU:0, one launch (start us, length us, event | category | flops | bytes accessed | tf_op | source)
XLA Modules:
  0.0 310.5 jit_solution(6108352041416000376)
XLA Ops:
  8.9 1.2 dynamic-slice.3
  10.8 0.7 bitcast_dynamic-update-slice_fusion
  11.5 0.8 bitcast_dynamic-update-slice_fusion.1
  12.2 9.9 %all-reduce.2 = (s32[4]{0:T(128)S(1)}, s32[64]{0:T(128)S(1)}) all-reduce(s32[4]{0:T(128)S(1)} %bitcast_dynamic-update-slice_fusion, s32[64]{0:T(128)S(1)} %bitcast_dynamic-update-slice_fusion.1), channel_id=1, replica_groups=mesh['row'=8,'col'=4] {'col'}, use_global_device_ids=true, to_apply=%add.1 | all-reduce | flops 68 | bytes 544
  24.2 1.3 slice.7
  25.5 1.7 convolution_convert_fusion
  27.9 1.1 slice.35
  30.4 0.7 gather_fusion
  31.1 8.8 %all-gather = s32[8,1,16]{2,1,0:T(1,128)S(1)} all-gather(s32[1,1,16]{2,1,0:T(1,128)S(1)} %bitcast.89), channel_id=1, replica_groups=mesh['row'=8,'col'=4] {'row'}, dimensions={0}, use_global_device_ids=true | all-gather | bytes 576 | tf_op jit(solution)/shard_map/all_gather | solution.py:19
  41.2 9.2 %all-gather.1 = s32[8,1,16]{2,1,0:T(1,128)S(1)} all-gather(s32[1,1,16]{2,1,0:T(1,128)S(1)} %bitcast.90), channel_id=1, replica_groups=mesh['row'=8,'col'=4] {'row'}, dimensions={0}, use_global_device_ids=true | all-gather | bytes 576 | tf_op jit(solution)/shard_map/all_gather | solution.py:20
  51.3 0.8 gather_fusion.4
  52.1 0.8 gather_fusion.5
  54.1 2.5 fusion.32
  56.8 21.7 %all-reduce.5.cloned.1.call-done = bf16[8,256,256]{2,0,1:T(8,128)(2,1)} async-done(((bf16[8,256,256]{2,0,1:T(8,128)(2,1)}), bf16[8,256,256]{2,0,1:T(8,128)(2,1)}) %all-reduce.5.cloned.1.call-update) | async-done | bytes 1048592 | tf_op jit(solution)/shard_map/psum | solution.py:44
  78.5 1.4 copy.21
  79.9 38.5 %all-gather.7.cloned.1.call-done = bf16[8,16,256,256]{3,2,1,0:T(8,128)(2,1)} async-done(((bf16[1,16,256,256]{3,2,1,0:T(8,128)(2,1)}), bf16[8,16,256,256]{3,2,1,0:T(8,128)(2,1)}) %all-gather.7.cloned.1.call-update) | async-done | bytes 16777232 | tf_op jit(solution)/shard_map/all_gather | solution.py:18
  118.5 10.4 %gather_fusion.3 = bf16[40,256,256]{2,1,0:T(8,128)(2,1)} fusion(bf16[128,256,256]{2,1,0:T(8,128)(2,1)} %bitcast.85, s32[1024]{0:T(1024)S(1)} %pad_clamp_fusion), kind=kCustom, calls=%fused_computation.5 | custom fusion | bytes 10485920 | tf_op jit(solution)/shard_map/jit(_take)/gather | solution.py:61
  128.9 71.6 %all-gather.5.cloned.1.call-done = bf16[1,32,256,256]{3,2,0,1:T(8,128)(2,1)} async-done(((bf16[1,8,256,256]{3,2,0,1:T(8,128)(2,1)}), bf16[1,32,256,256]{3,2,0,1:T(8,128)(2,1)}) %all-gather.5.cloned.1.call-update) | async-done | bytes 4194320 | tf_op jit(solution)/shard_map/all_gather | solution.py:25
  200.6 9.5 %fusion.3 = f32[40,256,256]{2,1,0:T(8,128)} fusion(bf16[8,256,256]{2,1,0:T(8,128)(2,1)S(1)} %copy.21, bf16[32,256,256]{2,1,0:T(8,128)(2,1)} %bitcast.91, bf16[40,256,256]{2,1,0:T(8,128)(2,1)} %gather_fusion.3, pred[40]{0:T(512)(128)(4,1)S(1)} %get-tuple-element.16), kind=kOutput, calls=%fused_computation.11 | convolution fusion | flops 1347420160 | bytes 20971560 | tf_op jit(solution)/shard_map/axy,ayz->axz/dot_general | solution.py:66
  210.0 18.0 %fusion.1 = f32[64,256,256]{2,0,1:T(8,128)S(1)} fusion(f32[40,256,256]{2,1,0:T(8,128)} %fusion.3, s32[40]{0:T(128)S(1)} %select_add_fusion, pred[40]{0:T(512)(128)(4,1)S(1)} %add_and_fusion), kind=kOutput, calls=%fused_computation.9 | convolution fusion | flops 2013271040 | bytes 27263176 | tf_op jit(solution)/shard_map/ap,axz->pxz/dot_general | solution.py:68
  228.1 9.9 %subtract_reduce_fusion = (f32[]{:T(128)}, bf16[64,256,256]{2,0,1:T(8,128)(2,1)}) fusion(f32[64,256,256]{2,0,1:T(8,128)S(1)} %fusion.1, bf16[16,256,256]{2,1,0:T(8,128)(2,1)S(1)} %bitcast.83, s32[16]{0:T(128)S(1)} %bitcast.88, pred[16]{0:T(512)(128)(4,1)S(1)} %iota_compare_fusion.6), kind=kOutput, calls=%fused_computation.6 | convolution fusion | flops 155191296 | bytes 27263060 | tf_op jit(solution)/shard_map/sp,sxz->pxz/dot_general | solution.py:71
  238.0 38.9 %psum.15 = f32[]{:T(128)} all-reduce(f32[]{:T(128)} %get-tuple-element.18), channel_id=1, replica_groups=mesh['row'=8,'col'=4] {'row','col'}, use_global_device_ids=true, to_apply=%region_5.7 | all-reduce | flops 1 | bytes 8 | tf_op jit(solution)/shard_map/psum | solution.py:78
  276.9 7.8 %copy.23 = bf16[2,256,32,256]{3,2,1,0:T(8,128)(2,1)} copy(bf16[2,256,32,256]{3,2,0,1:T(8,128)(2,1)} %bitcast.80) | data formatting | bytes 16777216 | tf_op jit(solution)/shard_map/convert_element_type | solution.py:81
  284.7 16.6 %copy.25 = bf16[64,8,32,256]{3,1,2,0:T(8,128)(2,1)} copy(bf16[64,8,32,256]{3,2,1,0:T(8,128)(2,1)} %bitcast.81) | data formatting | bytes 16777216
  (50 shorter events, 7.1 us)
Async XLA Ops:
  8.0 19.9 %copy-start = (bf16[1,16,256,256]{3,2,1,0:T(8,128)(2,1)S(1)}, bf16[1,16,256,256]{3,2,1,0:T(8,128)(2,1)}, u32[]{:S(2)}) copy-start(bf16[1,16,256,256]{3,2,1,0:T(8,128)(2,1)} %param.8) | copy-start | bytes 6291460
  8.0 70.5 %all-reduce.5.cloned.1.call-start = ((), (), s32[]{:S(2)}) async-start(), calls=%async_computation.1 | async-start | bytes 2097152 | tf_op jit(solution)/shard_map/psum | solution.py:44
  25.5 5.6 %copy-start.2 = (s32[1,16]{1,0:T(1,128)S(1)}, s32[1,16]{1,0:T(1,128)}, u32[]{:S(2)}) copy-start(s32[1,16]{1,0:T(1,128)} %param.12) | copy-start | bytes 196
  25.5 15.7 %copy-start.3 = (s32[1,16]{1,0:T(1,128)S(1)}, s32[1,16]{1,0:T(1,128)}, u32[]{:S(2)}) copy-start(s32[1,16]{1,0:T(1,128)} %param.13) | copy-start | bytes 196
  27.2 91.3 %all-gather.7.cloned.1.call-start = ((), (), s32[]{:S(2)}) async-start(), calls=%async_computation.2 | async-start | bytes 18874368 | tf_op jit(solution)/shard_map/all_gather | solution.py:18
  27.8 172.7 %all-gather.5.cloned.1.call-start = ((), (), s32[]{:S(2)}) async-start(), calls=%async_computation | async-start | bytes 5242880 | tf_op jit(solution)/shard_map/all_gather | solution.py:25
  210.0 18.0 %copy-start.1 = (s32[1,16]{1,0:T(1,128)S(1)}, s32[1,16]{1,0:T(1,128)}, u32[]{:S(2)}) copy-start(s32[1,16]{1,0:T(1,128)} %param.9) | copy-start | bytes 196
Sparse Core Ops, SparseCore 0:
  27.3 51.1 all-reduce.4
Sparse Core Ops, SparseCore 1:
  29.6 88.8 all-gather.6
  119.9 80.6 all-gather.4
where the time goes:
time: 311 us
  waiting for transfers between devices  132 us (42%)
  blocking collectives  66.8 us (21%)
  local copies, waits for them, and re-layouts  46.8 us (15%)
  matrix products  39.1 us (13%)
  between operations  19.5 us (6%)
  other arithmetic  5.76 us (2%)
    all_gather x1, waiting for transfers between devices, on_device(): lax.all_gather(band_tiles[:, :half], 'col', axis=1, tiled=True)  71.6 us
    psum x1, blocking collectives, on_device(): total = lax.psum(jnp.sum(expanded - base), ('row', 'col'))  38.9 us
    all_gather x1, waiting for transfers between devices, on_device(): lax.all_gather(matrix_tiles, 'row', axis=0, tiled=True)  38.5 us
    psum x1, waiting for transfers between devices, on_device(): spilled = lax.psum(packed.astype(jnp.bfloat16), 'col')  21.7 us
    unnamed x14, local copies, waits for them, and re-layouts  19.3 us
    dot_general x1, matrix products, on_device(): jnp.einsum('ap,axz->pxz', weights, product, precision=lax.Precision.HIGHEST)  18 us
    gather x1, local copies, waits for them, and re-layouts, on_device(): picked = jnp.take(flat_tiles, k_glob, axis=0)  10.4 us
    dot_general x1, matrix products, on_device(): jnp.einsum('sp,sxz->pxz', own_w, band_tiles[0], preferred_element_type=jn...  9.92 us
  transfers between devices with their start and end apart: 3, of which 3 were waited for; matrix products, arithmetic and copies ran while one was open for 7% of the time, Pallas kernels for 0%

commit v1 on v0

--- a/solution.py
+++ b/solution.py
@@ -41,7 +41,9 @@
     packed = jnp.einsum(
         "qs,sxy->qxy", place_w, band_tiles[0, half:], preferred_element_type=jnp.float32
     )
-    spilled = lax.psum(packed.astype(jnp.bfloat16), "col")
+    block_2 = packed.astype(jnp.bfloat16)
+    terms = lax.all_gather(block_2, "col")
+    spilled = jnp.sum(terms, axis=0)
     holder = jnp.sum((ending[None, :] <= pack_spot[:, None]).astype(jnp.int32), axis=1)
     holder = jnp.clip(holder, 0, n_col - 1)
     spill_slot = jnp.clip(half + pack_spot - jnp.take(before, holder), 0, slots_own - 1)

time: 311 us -> 388 us (1.25)
  waiting for transfers between devices: 132 us -> 209 us
    all_gather x0 -> x1, waiting for transfers between devices: none -> 50.3 us  [on_device(): terms = lax.all_gather(block_2, 'col')]
    all_gather x1, waiting for transfers between devices: 38.5 us -> 86.1 us  [on_device(): lax.all_gather(matrix_tiles, 'row', axis=0, tiled=True)]
    psum x1 -> x0, waiting for transfers between devices: 21.7 us -> none  [on_device(): spilled = lax.psum(packed.astype(jnp.bfloat16), 'col')]
where the time goes in v1:
time: 388 us; the launch traced here: 387 us
  waiting for transfers between devices  209 us (54%)
  blocking collectives  66.4 us (17%)
  local copies, waits for them, and re-layouts  45.8 us (12%)
  matrix products  38.9 us (10%)
  between operations  17.8 us (5%)
  other arithmetic  9.6 us (2%)
    all_gather x1, waiting for transfers between devices, on_device(): lax.all_gather(matrix_tiles, 'row', axis=0, tiled=True)  86.1 us
    all_gather x1, waiting for transfers between devices, on_device(): lax.all_gather(band_tiles[:, :half], 'col', axis=1, tiled=True)  71.7 us
    all_gather x1, waiting for transfers between devices, on_device(): terms = lax.all_gather(block_2, 'col')  50.3 us
    psum x1, blocking collectives, on_device(): total = lax.psum(jnp.sum(expanded - base), ('row', 'col'))  39 us
    unnamed x14, local copies, waits for them, and re-layouts  19.3 us
    dot_general x1, matrix products, on_device(): jnp.einsum('ap,axz->pxz', weights, product, precision=lax.Precision.HIGHEST)  18 us
    gather x1, local copies, waits for them, and re-layouts, on_device(): picked = jnp.take(flat_tiles, k_glob, axis=0)  10.6 us
    unnamed x1, blocking collectives  9.92 us
  transfers between devices with their start and end apart: 3, of which 3 were waited for; matrix products, arithmetic and copies ran while one was open for 7% of the time, Pallas kernels for 0%

profile of v1, /device:TPU:0, one launch (start us, length us, event | category | flops | bytes accessed | tf_op | source)
XLA Modules:
  0.0 387.5 jit_solution(2758489327493369942)
XLA Ops:
  8.0 1.2 dynamic-slice.3
  10.6 0.8 bitcast_dynamic-update-slice_fusion.1
  11.4 9.9 %all-reduce.2 = (s32[4]{0:T(128)S(1)}, s32[64]{0:T(128)S(1)}) all-reduce(s32[4]{0:T(128)S(1)} %bitcast_dynamic-update-slice_fusion, s32[64]{0:T(128)S(1)} %bitcast_dynamic-update-slice_fusion.1), channel_id=1, replica_groups=mesh['row'=8,'col'=4] {'col'}, use_global_device_ids=true, to_apply=%add.1 | all-reduce | flops 68 | bytes 544
  23.4 1.3 slice.7
  24.7 1.7 convolution_convert_fusion
  26.5 0.7 all-gather.9.cloned.1.call-update
  27.3 1.1 slice.35
  29.9 0.7 gather_fusion
  30.6 8.8 %all-gather.1 = s32[8,1,16]{2,1,0:T(1,128)S(1)} all-gather(s32[1,1,16]{2,1,0:T(1,128)S(1)} %bitcast.91), channel_id=1, replica_groups=mesh['row'=8,'col'=4] {'row'}, dimensions={0}, use_global_device_ids=true | all-gather | bytes 576 | tf_op jit(solution)/shard_map/all_gather | solution.py:19
  40.6 8.8 %all-gather.2 = s32[8,1,16]{2,1,0:T(1,128)S(1)} all-gather(s32[1,1,16]{2,1,0:T(1,128)S(1)} %bitcast.92), channel_id=1, replica_groups=mesh['row'=8,'col'=4] {'row'}, dimensions={0}, use_global_device_ids=true | all-gather | bytes 576 | tf_op jit(solution)/shard_map/all_gather | solution.py:20
  50.3 0.8 gather_fusion.4
  51.1 0.8 gather_fusion.5
  53.2 2.7 fusion.32
  56.1 50.3 %all-gather.11.cloned.1.call-done = bf16[32,256,256]{2,0,1:T(8,128)(2,1)} async-done(((bf16[8,256,256]{2,0,1:T(8,128)(2,1)}), bf16[32,256,256]{2,0,1:T(8,128)(2,1)}) %all-gather.11.cloned.1.call-update) | async-done | bytes 4194320 | tf_op jit(solution)/shard_map/all_gather | solution.py:45
  106.4 3.6 bitcast_reduce_fusion
  110.1 86.1 %all-gather.9.cloned.1.call-done = bf16[8,16,256,256]{3,2,1,0:T(8,128)(2,1)} async-done(((bf16[1,16,256,256]{3,2,1,0:T(8,128)(2,1)}), bf16[8,16,256,256]{3,2,1,0:T(8,128)(2,1)}) %all-gather.9.cloned.1.call-update) | async-done | bytes 16777232 | tf_op jit(solution)/shard_map/all_gather | solution.py:18
  196.2 10.6 %gather_fusion.3 = bf16[40,256,256]{2,1,0:T(8,128)(2,1)} fusion(bf16[128,256,256]{2,1,0:T(8,128)(2,1)} %bitcast.87, s32[1024]{0:T(1024)S(1)} %pad_clamp_fusion), kind=kCustom, calls=%fused_computation.5 | custom fusion | bytes 10485920 | tf_op jit(solution)/shard_map/jit(_take)/gather | solution.py:63
  206.8 71.7 %all-gather.7.cloned.1.call-done = bf16[1,32,256,256]{3,2,0,1:T(8,128)(2,1)} async-done(((bf16[1,8,256,256]{3,2,0,1:T(8,128)(2,1)}), bf16[1,32,256,256]{3,2,0,1:T(8,128)(2,1)}) %all-gather.7.cloned.1.call-update) | async-done | bytes 4194320 | tf_op jit(solution)/shard_map/all_gather | solution.py:25
  278.5 9.5 %fusion.3 = f32[40,256,256]{2,1,0:T(8,128)} fusion(bf16[8,256,256]{2,1,0:T(8,128)(2,1)S(1)} %copy.23, bf16[32,256,256]{2,1,0:T(8,128)(2,1)} %bitcast.93, bf16[40,256,256]{2,1,0:T(8,128)(2,1)} %gather_fusion.3, pred[40]{0:T(512)(128)(4,1)S(1)} %get-tuple-element.16), kind=kOutput, calls=%fused_computation.11 | convolution fusion | flops 1347420160 | bytes 20971560 | tf_op jit(solution)/shard_map/axy,ayz->axz/dot_general | solution.py:68
  288.0 18.0 %fusion.1 = f32[64,256,256]{2,0,1:T(8,128)S(1)} fusion(f32[40,256,256]{2,1,0:T(8,128)} %fusion.3, s32[40]{0:T(128)S(1)} %select_add_fusion, pred[40]{0:T(512)(128)(4,1)S(1)} %add_and_fusion), kind=kOutput, calls=%fused_computation.9 | convolution fusion | flops 2013271040 | bytes 27263176 | tf_op jit(solution)/shard_map/ap,axz->pxz/dot_general | solution.py:70
  306.1 9.7 %subtract_reduce_fusion = (f32[]{:T(128)}, bf16[64,256,256]{2,0,1:T(8,128)(2,1)}) fusion(f32[64,256,256]{2,0,1:T(8,128)S(1)} %fusion.1, bf16[16,256,256]{2,1,0:T(8,128)(2,1)S(1)} %bitcast.85, s32[16]{0:T(128)S(1)} %bitcast.90, pred[16]{0:T(512)(128)(4,1)S(1)} %iota_compare_fusion.6), kind=kOutput, calls=%fused_computation.6 | convolution fusion | flops 155191296 | bytes 27263060 | tf_op jit(solution)/shard_map/sp,sxz->pxz/dot_general | solution.py:73
  315.8 39.0 %psum.7 = f32[]{:T(128)} all-reduce(f32[]{:T(128)} %get-tuple-element.18), channel_id=1, replica_groups=mesh['row'=8,'col'=4] {'row','col'}, use_global_device_ids=true, to_apply=%region_5.7 | all-reduce | flops 1 | bytes 8 | tf_op jit(solution)/shard_map/psum | solution.py:80
  354.7 7.8 %copy.25 = bf16[2,256,32,256]{3,2,1,0:T(8,128)(2,1)} copy(bf16[2,256,32,256]{3,2,0,1:T(8,128)(2,1)} %bitcast.82) | data formatting | bytes 16777216 | tf_op jit(solution)/shard_map/convert_element_type | solution.py:83
  362.6 16.6 %copy.27 = bf16[64,8,32,256]{3,1,2,0:T(8,128)(2,1)} copy(bf16[64,8,32,256]{3,2,1,0:T(8,128)(2,1)} %bitcast.83) | data formatting | bytes 16777216
  (51 shorter events, 7.7 us)
Async XLA Ops:
  7.2 20.1 %copy-start = (bf16[1,16,256,256]{3,2,1,0:T(8,128)(2,1)S(1)}, bf16[1,16,256,256]{3,2,1,0:T(8,128)(2,1)}, u32[]{:S(2)}) copy-start(bf16[1,16,256,256]{3,2,1,0:T(8,128)(2,1)} %param.8) | copy-start | bytes 6291460
  7.2 99.2 %all-gather.11.cloned.1.call-start = ((), (), s32[]{:S(2)}) async-start(), calls=%async_computation.2 | async-start | bytes 5242880 | tf_op jit(solution)/shard_map/all_gather | solution.py:45
  24.7 5.9 %copy-start.2 = (s32[1,16]{1,0:T(1,128)S(1)}, s32[1,16]{1,0:T(1,128)}, u32[]{:S(2)}) copy-start(s32[1,16]{1,0:T(1,128)} %param.12) | copy-start | bytes 196
  24.7 15.9 %copy-start.3 = (s32[1,16]{1,0:T(1,128)S(1)}, s32[1,16]{1,0:T(1,128)}, u32[]{:S(2)}) copy-start(s32[1,16]{1,0:T(1,128)} %param.13) | copy-start | bytes 196
  26.4 169.8 %all-gather.9.cloned.1.call-start = ((), (), s32[]{:S(2)}) async-start(), calls=%async_computation.1 | async-start | bytes 18874368 | tf_op jit(solution)/shard_map/all_gather | solution.py:18
  27.2 251.3 %all-gather.7.cloned.1.call-start = ((), (), s32[]{:S(2)}) async-start(), calls=%async_computation | async-start | bytes 5242880 | tf_op jit(solution)/shard_map/all_gather | solution.py:25
  288.0 18.0 %copy-start.1 = (s32[1,16]{1,0:T(1,128)S(1)}, s32[1,16]{1,0:T(1,128)}, u32[]{:S(2)}) copy-start(s32[1,16]{1,0:T(1,128)} %param.9) | copy-start | bytes 196
Sparse Core Ops, SparseCore 0:
  26.6 79.7 all-gather.10
  108.2 87.9 all-gather.8
  197.8 80.7 all-gather.6
